TPU v7x, 32 devices: a whole 2x2x4 slice. The times are simulated.
32 devices in a mesh: ep: 4 (over z), fsdp: 8 (over y, x, core).
Axes of the slice: x: 2, y: 2, z: 4, core: 2. Of those that a mesh axis runs over, the one named last changes fastest.
Arguments:
- train_gate: float32 [64, 2048, 1408], P('ep', 'fsdp'), may hold values from -0.1875 to 0.1875
- train_up: float32 [64, 2048, 1408], P('ep', 'fsdp'), may hold values from -0.1875 to 0.1875
- train_down: float32 [64, 1408, 2048], P('ep', None, 'fsdp'), may hold values from -0.21875 to 0.21875
- router_weight: float32 [2048, 64], P('fsdp', 'ep'), may hold values from -0.125 to 0.125
- router_gain: float32 [2048], P('fsdp'), may hold values from 0.25 to 1.75
Outputs:
- ready_gate: bfloat16 [64, 2048, 1408], P('ep', None, 'fsdp')
- ready_up: bfloat16 [64, 2048, 1408], P('ep', None, 'fsdp')
- ready_down: bfloat16 [64, 1408, 2048], P('ep', 'fsdp')
- scale_gate: float32 [64, 1408], P('ep', 'fsdp')
- scale_up: float32 [64, 1408], P('ep', 'fsdp')
- scale_down: float32 [64, 1408], P('ep', 'fsdp')
- serve_router: bfloat16 [2048, 64], replicated
All inputs are finite; a program needn't handle non-finite values.
Results may differ from a plain program's by a relative error of at most 0.001.
Values may be sent and summed in bfloat16 or wider, within the bound.
A program may use at most 192 MiB of HBM per device.

v0:
```python
import jax
import jax.numpy as jnp
from jax import lax
from jax.sharding import PartitionSpec as P


def body(train_gate, train_up, train_down, router_weight, router_gain):
    total_gate, total_up, total_down = lax.psum(
        (
            jnp.sum(train_gate * train_gate, axis=1),
            jnp.sum(train_up * train_up, axis=1),
            jnp.sum(train_down * train_down, axis=2),
        ),
        "fsdp",
    )
    scale_gate = jnp.sqrt(total_gate)
    scale_up = jnp.sqrt(total_up)
    scale_down = jnp.sqrt(total_down)
    narrow_gate, narrow_up, narrow_down = (
        (train_gate / jnp.expand_dims(scale_gate, 1)).astype(jnp.bfloat16),
        (train_up / jnp.expand_dims(scale_up, 1)).astype(jnp.bfloat16),
        (train_down / jnp.expand_dims(scale_down, 2)).astype(jnp.bfloat16),
    )
    ready_gate, ready_up = (
        lax.all_to_all(narrow_gate, "fsdp", split_axis=2, concat_axis=1, tiled=True),
        lax.all_to_all(narrow_up, "fsdp", split_axis=2, concat_axis=1, tiled=True),
    )
    ready_down = lax.all_to_all(narrow_down, "fsdp", split_axis=1, concat_axis=2, tiled=True)
    scale_gate = lax.dynamic_slice_in_dim(
        scale_gate, lax.axis_index("fsdp") * ready_gate.shape[2], ready_gate.shape[2], axis=1
    )
    scale_up = lax.dynamic_slice_in_dim(
        scale_up, lax.axis_index("fsdp") * ready_up.shape[2], ready_up.shape[2], axis=1
    )
    scale_down = lax.dynamic_slice_in_dim(
        scale_down, lax.axis_index("fsdp") * ready_down.shape[1], ready_down.shape[1], axis=1
    )
    part_router = (router_weight * router_gain[:, None]).astype(jnp.bfloat16)
    row_router = lax.all_gather(part_router, "fsdp", axis=0, tiled=True)
    serve_router = lax.all_gather(row_router, "ep", axis=1, tiled=True)
    return (ready_gate, ready_up, ready_down, scale_gate, scale_up, scale_down, serve_router)


def solution(mesh):
    return jax.shard_map(
        body,
        mesh=mesh,
        in_specs=(
            P("ep", "fsdp", None),
            P("ep", "fsdp", None),
            P("ep", None, "fsdp"),
            P("fsdp", "ep"),
            P("fsdp"),
        ),
        out_specs=(
            P("ep", None, "fsdp"),
            P("ep", None, "fsdp"),
            P("ep", "fsdp", None),
            P("ep", "fsdp"),
            P("ep", "fsdp"),
            P("ep", "fsdp"),
            P(),
        ),
        check_vma=False,
    )
```

profile of v0, /device:TPU:0, one launch (start us, length us, event | category | flops | bytes accessed | tf_op | source)
XLA Modules:
  0.0 618.1 jit_solution(2208627624309375978)
XLA Ops:
  7.2 9.2 %multiply_reduce_fusion = f32[16,1408]{1,0:T(8,128)} fusion(f32[16,1408,256]{2,1,0:T(8,128)} %param.7), kind=kLoop, calls=%fused_computation.2 | loop fusion | flops 11511808 | bytes 23158784 | tf_op jit(solution)/shard_map/reduce_sum | solution.py:12
  16.4 5.0 copy-done
  21.4 11.0 %multiply_reduce_fusion.1 = (f32[16,1408]{1,0:T(8,128)}, f32[16,1408]{1,0:T(8,128)}) fusion(f32[16,256,1408]{2,1,0:T(8,128)S(1)} %copy-done, f32[16,256,1408]{2,1,0:T(8,128)} %param.5), kind=kLoop, calls=%fused_computation.4 | loop fusion | flops 23023616 | bytes 46317568 | tf_op jit(solution)/shard_map/reduce_sum | solution.py:11
  32.5 23.7 %copy.28 = f32[16,256,1408]{1,0,2:T(8,128)} copy(f32[16,256,1408]{2,1,0:T(8,128)} %param.6) | data formatting | bytes 46137344 | tf_op args[1]
  56.2 32.6 %all-reduce.3.cloned.1.call-done = (f32[16,1408]{1,0:T(8,128)}, f32[16,1408]{1,0:T(8,128)}, f32[16,1408]{1,0:T(8,128)}) async-done(((f32[16,1408]{1,0:T(8,128)}, f32[16,1408]{1,0:T(8,128)}, f32[16,1408]{1,0:T(8,128)}), (f32[16,1408]{1,0:T(8,128)}, f32[16,1408]{1,0:T(8,128)}, f32[16,1408]{1,0:T(8,128)})) %all-reduce.3.cloned.1.call-update) | async-done | bytes 270352 | tf_op jit(solution)/shard_map/psum | solution.py:8
  88.8 0.9 sqrt.10
  90.0 14.2 %divide_convert_fusion = bf16[16,256,1408]{1,0,2:T(8,128)(2,1)} fusion(f32[16,256,1408]{1,0,2:T(8,128)} %copy.28, f32[16,1408]{0,1:T(8,128)S(1)} %copy.27), kind=kLoop, calls=%fused_computation.3 | loop fusion | flops 11534336 | bytes 34693120 | tf_op jit(solution)/shard_map/convert_element_type | solution.py:21
  104.2 5.2 all-to-all-start.1
  109.5 23.7 %copy.24 = f32[16,256,1408]{1,0,2:T(8,128)} copy(f32[16,256,1408]{2,1,0:T(8,128)} %param.5) | data formatting | bytes 46137344 | tf_op args[0]
  133.5 14.2 %divide_convert_fusion.1 = bf16[16,256,1408]{1,0,2:T(8,128)(2,1)} fusion(f32[16,256,1408]{1,0,2:T(8,128)} %copy.24, f32[16,1408]{0,1:T(8,128)S(1)} %copy.23), kind=kLoop, calls=%fused_computation.5 | loop fusion | flops 11534336 | bytes 34693120 | tf_op jit(solution)/shard_map/convert_element_type | solution.py:20
  147.7 89.5 %all-to-all-done.1 = bf16[16,256,1408]{1,0,2:T(8,128)(2,1)} async-done(((bf16[16,256,1408]{1,0,2:T(8,128)(2,1)}), bf16[16,256,1408]{1,0,2:T(8,128)(2,1)}, u32[]{:S(2)}, u32[]{:S(2)}) %all-to-all-start.1) | async-done | bytes 11534368 | tf_op jit(solution)/shard_map/all_to_all | solution.py:26
  237.2 5.3 all-to-all-start
  242.8 32.6 %fusion = bf16[16,1408,256]{2,0,1:T(8,128)(2,1)} fusion(f32[16,1408,256]{2,1,0:T(8,128)} %param.7, f32[16,1408]{0,1:T(8,128)S(1)} %copy.31), kind=kLoop, calls=%fused_computation.1 | loop fusion | flops 11534336 | bytes 34693120 | tf_op jit(solution)/shard_map/convert_element_type | solution.py:22
  275.4 94.8 %all-to-all-done = bf16[16,256,1408]{1,0,2:T(8,128)(2,1)} async-done(((bf16[16,256,1408]{1,0,2:T(8,128)(2,1)}), bf16[16,256,1408]{1,0,2:T(8,128)(2,1)}, u32[]{:S(2)}, u32[]{:S(2)}) %all-to-all-start) | async-done | bytes 11534368 | tf_op jit(solution)/shard_map/all_to_all | solution.py:25
  370.2 5.3 all-to-all-start.2
  375.5 130.9 %all_gather.6 = bf16[2048,16]{0,1:T(8,128)(2,1)S(1)} all-gather(bf16[256,16]{0,1:T(8,128)(2,1)S(1)} %multiply_convert_fusion), channel_id=1, replica_groups=mesh['ep'=4,'fsdp'=8] {'fsdp'}, dimensions={0}, use_global_device_ids=true | all-gather | bytes 73728 | tf_op jit(solution)/shard_map/all_gather | solution.py:39
  506.4 14.2 %all_gather.7 = bf16[2048,64]{0,1:T(8,128)(2,1)S(1)} all-gather(bf16[2048,16]{0,1:T(8,128)(2,1)S(1)} %all_gather.6), channel_id=1, replica_groups=mesh['ep'=4,'fsdp'=8] {'ep'}, dimensions={1}, use_global_device_ids=true | all-gather | bytes 327680 | tf_op jit(solution)/shard_map/all_gather | solution.py:40
  522.6 11.3 %copy.30 = bf16[16,8,256,176]{2,1,3,0:T(8,128)(2,1)} copy(bf16[16,8,256,176]{2,0,3,1:T(8,128)(2,1)} %bitcast.5) | data formatting | bytes 23068672 | tf_op jit(solution)/shard_map/all_to_all | solution.py:26
  534.0 18.0 %all_to_all.46 = bf16[16,2048,176]{1,2,0:T(8,128)(2,1)} reshape(bf16[16,8,256,176]{2,1,3,0:T(8,128)(2,1)} %copy.30) | data formatting | bytes 23068672 | tf_op jit(solution)/shard_map/all_to_all | solution.py:26
  551.9 11.3 %copy.26 = bf16[16,8,256,176]{2,1,3,0:T(8,128)(2,1)} copy(bf16[16,8,256,176]{2,0,3,1:T(8,128)(2,1)} %bitcast.2) | data formatting | bytes 23068672 | tf_op jit(solution)/shard_map/all_to_all | solution.py:25
  563.3 18.0 %all_to_all.42 = bf16[16,2048,176]{1,2,0:T(8,128)(2,1)} reshape(bf16[16,8,256,176]{2,1,3,0:T(8,128)(2,1)} %copy.26) | data formatting | bytes 23068672 | tf_op jit(solution)/shard_map/all_to_all | solution.py:25
  581.2 11.3 %copy.33 = bf16[16,176,8,256]{3,2,1,0:T(8,128)(2,1)} copy(bf16[16,176,8,256]{3,0,1,2:T(8,128)(2,1)} %bitcast.7) | data formatting | bytes 23068672 | tf_op jit(solution)/shard_map/all_to_all | solution.py:28
  592.5 18.0 %all_to_all.50 = bf16[16,176,2048]{2,1,0:T(8,128)(2,1)} reshape(bf16[16,176,8,256]{3,2,1,0:T(8,128)(2,1)} %copy.33) | data formatting | bytes 23068672 | tf_op jit(solution)/shard_map/all_to_all | solution.py:28
  610.5 0.7 copy.43
  (21 shorter events, 3.0 us)
Async XLA Ops:
  7.2 81.6 %all-reduce.3.cloned.1.call-start = ((), (), s32[]{:S(2)}) async-start(), calls=%async_computation.3 | async-start | bytes 540672 | tf_op jit(solution)/shard_map/psum | solution.py:8
  7.2 14.2 %copy-start = (f32[16,256,1408]{2,1,0:T(8,128)S(1)}, f32[16,256,1408]{2,1,0:T(8,128)}, u32[]{:S(2)}) copy-start(f32[16,256,1408]{2,1,0:T(8,128)} %param.6) | copy-start | bytes 69206016
  104.2 133.0 %all-to-all-start.1 = ((bf16[16,256,1408]{1,0,2:T(8,128)(2,1)}), bf16[16,256,1408]{1,0,2:T(8,128)(2,1)}, u32[]{:S(2)}, u32[]{:S(2)}) async-start(bf16[16,256,1408]{1,0,2:T(8,128)(2,1)} %divide_convert_fusion), calls=%async_computation.1 | async-start | bytes 23068672 | tf_op jit(solution)/shard_map/all_to_all | solution.py:26
  109.5 23.7 %copy-start.2 = (f32[16,1408]{1,0:T(8,128)S(1)}, f32[16,1408]{1,0:T(8,128)}, u32[]{:S(2)}) copy-start(f32[16,1408]{1,0:T(8,128)} %get-tuple-element.7) | copy-start | bytes 270340
  133.5 109.0 %copy-start.1 = (f32[16,1408]{1,0:T(8,128)S(1)}, f32[16,1408]{1,0:T(8,128)}, u32[]{:S(2)}) copy-start(f32[16,1408]{1,0:T(8,128)} %get-tuple-element.9) | copy-start | bytes 270340
  237.2 133.0 %all-to-all-start = ((bf16[16,256,1408]{1,0,2:T(8,128)(2,1)}), bf16[16,256,1408]{1,0,2:T(8,128)(2,1)}, u32[]{:S(2)}, u32[]{:S(2)}) async-start(bf16[16,256,1408]{1,0,2:T(8,128)(2,1)} %divide_convert_fusion.1), calls=%async_computation | async-start | bytes 23068672 | tf_op jit(solution)/shard_map/all_to_all | solution.py:25
  242.8 132.7 %copy-start.3 = (f32[256,16]{0,1:T(8,128)S(1)}, f32[256,16]{0,1:T(8,128)}, u32[]{:S(2)}) copy-start(f32[256,16]{0,1:T(8,128)} %param.8) | copy-start | bytes 49156
  242.8 132.7 %copy-start.4 = (f32[256]{0:T(256)S(1)}, f32[256]{0:T(256)}, u32[]{:S(2)}) copy-start(f32[256]{0:T(256)} %param.9) | copy-start | bytes 3076
  370.2 211.0 %all-to-all-start.2 = ((bf16[16,1408,256]{2,0,1:T(8,128)(2,1)}), bf16[16,1408,256]{2,0,1:T(8,128)(2,1)}, u32[]{:S(2)}, u32[]{:S(2)}) async-start(bf16[16,1408,256]{2,0,1:T(8,128)(2,1)} %fusion), calls=%async_computation.2 | async-start | bytes 23068672 | tf_op jit(solution)/shard_map/all_to_all | solution.py:28
Sparse Core Ops, SparseCore 0:
  32.6 56.1 all-reduce.2
where the time goes:
time: 621 us; the launch traced here: 618 us
  waiting for transfers between devices  217 us (35%)
  local copies, waits for them, and re-layouts  145 us (23%)
  blocking collectives  145 us (23%)
  other arithmetic  81.3 us (13%)
  starting transfers between devices  15.8 us (3%)
  between operations  14.2 us (2%)
    all_gather x1, blocking collectives, body(): row_router = lax.all_gather(part_router, 'fsdp', axis=0, tiled=True)  131 us
    all_to_all x1, waiting for transfers between devices, body(): lax.all_to_all(narrow_gate, 'fsdp', split_axis=2, concat_axis=1, tiled=True)  94.8 us
    all_to_all x1, waiting for transfers between devices, body(): lax.all_to_all(narrow_up, 'fsdp', split_axis=2, concat_axis=1, tiled=True)  89.5 us
    unnamed x13, local copies, waits for them, and re-layouts  53.2 us
    psum x1, waiting for transfers between devices, body(): lax.psum((jnp.sum(train_gate * train_gate, axis=1), jnp.sum(train_up * tr...  32.6 us
    convert_element_type x1, other arithmetic, body(): (train_down / jnp.expand_dims(scale_down, 2)).astype(jnp.bfloat16)  32.6 us
    all_to_all x2, local copies, waits for them, and re-layouts, body(): lax.all_to_all(narrow_up, 'fsdp', split_axis=2, concat_axis=1, tiled=True)  29.3 us
    all_to_all x2, local copies, waits for them, and re-layouts, body(): lax.all_to_all(narrow_gate, 'fsdp', split_axis=2, concat_axis=1, tiled=True)  29.3 us
  transfers between devices with their start and end apart: 4, of which 3 were waited for; matrix products, arithmetic and copies ran while one was open for 19% of the time, Pallas kernels for 0%

commit v1 on v0

--- a/solution.py
+++ b/solution.py
@@ -36,7 +36,12 @@
         scale_down, lax.axis_index("fsdp") * ready_down.shape[1], ready_down.shape[1], axis=1
     )
     part_router = (router_weight * router_gain[:, None]).astype(jnp.bfloat16)
-    row_router = lax.all_gather(part_router, "fsdp", axis=0, tiled=True)
+    ring = [part_router]
+    for hop in range(7):
+        ring.append(lax.ppermute(ring[-1], "fsdp", [(dev, (dev + 1) % 8) for dev in range(8)]))
+    row_router = jnp.roll(
+        jnp.concatenate(ring[::-1], axis=0), (lax.axis_index("fsdp") + 1) * ring[0].shape[0], axis=0
+    )
     serve_router = lax.all_gather(row_router, "ep", axis=1, tiled=True)
     return (ready_gate, ready_up, ready_down, scale_gate, scale_up, scale_down, serve_router)
 

time: 621 us -> 642 us (1.034)
  waiting for transfers between devices: 217 us -> 368 us
  blocking collectives: 145 us -> 14.6 us
    ppermute x0 -> x7, waiting for transfers between devices: none -> 151 us  [body(): lax.ppermute(ring[-1], 'fsdp', [(dev, (dev + 1) % 8) for dev in range(8)])]
    all_gather x1 -> x0, blocking collectives: 131 us -> none  [body(): row_router = lax.all_gather(part_router, 'fsdp', axis=0, tiled=True)]
    unnamed x13 -> x27, local copies, waits for them, and re-layouts: 53.2 us -> 53.2 us
  transfers between devices with their start and end apart: 4 -> 11, of which waited for: 3 -> 10; matrix products, arithmetic and copies ran while one was open for 19% -> 19% of each run, Pallas kernels for 0% -> 0%
where the time goes in v1:
time: 642 us; the launch traced here: 639 us
  waiting for transfers between devices  368 us (57%)
  local copies, waits for them, and re-layouts  145 us (23%)
  other arithmetic  81.2 us (13%)
  starting transfers between devices  16.2 us (3%)
  blocking collectives  14.6 us (2%)
  between operations  14.3 us (2%)
    ppermute x7, waiting for transfers between devices, body(): lax.ppermute(ring[-1], 'fsdp', [(dev, (dev + 1) % 8) for dev in range(8)])  151 us
    all_to_all x1, waiting for transfers between devices, body(): lax.all_to_all(narrow_up, 'fsdp', split_axis=2, concat_axis=1, tiled=True)  94.8 us
    all_to_all x1, waiting for transfers between devices, body(): lax.all_to_all(narrow_gate, 'fsdp', split_axis=2, concat_axis=1, tiled=True)  89.5 us
    unnamed x27, local copies, waits for them, and re-layouts  53.2 us
    psum x1, waiting for transfers between devices, body(): lax.psum((jnp.sum(train_gate * train_gate, axis=1), jnp.sum(train_up * tr...  32.6 us
    convert_element_type x1, other arithmetic, body(): (train_down / jnp.expand_dims(scale_down, 2)).astype(jnp.bfloat16)  32.6 us
    all_to_all x2, local copies, waits for them, and re-layouts, body(): lax.all_to_all(narrow_down, 'fsdp', split_axis=1, concat_axis=2, tiled=True)  29.4 us
    all_to_all x2, local copies, waits for them, and re-layouts, body(): lax.all_to_all(narrow_gate, 'fsdp', split_axis=2, concat_axis=1, tiled=True)  29.3 us
  transfers between devices with their start and end apart: 11, of which 10 were waited for; matrix products, arithmetic and copies ran while one was open for 19% of the time, Pallas kernels for 0%

profile of v1, /device:TPU:0, one launch (start us, length us, event | category | flops | bytes accessed | tf_op | source)
XLA Modules:
  0.0 638.9 jit_solution(10881935652031790808)
XLA Ops:
  7.2 9.2 %multiply_reduce_fusion = f32[16,1408]{1,0:T(8,128)} fusion(f32[16,1408,256]{2,1,0:T(8,128)} %param.7), kind=kLoop, calls=%fused_computation.2 | loop fusion | flops 11511808 | bytes 23158784 | tf_op jit(solution)/shard_map/reduce_sum | solution.py:12
  16.4 5.0 copy-done
  21.4 11.0 %multiply_reduce_fusion.1 = (f32[16,1408]{1,0:T(8,128)}, f32[16,1408]{1,0:T(8,128)}) fusion(f32[16,256,1408]{2,1,0:T(8,128)} %param.6, f32[16,256,1408]{2,1,0:T(8,128)S(1)} %copy-done), kind=kLoop, calls=%fused_computation.4 | loop fusion | flops 23023616 | bytes 46317568 | tf_op jit(solution)/shard_map/reduce_sum | solution.py:11
  32.5 23.7 %copy.24 = f32[16,256,1408]{1,0,2:T(8,128)} copy(f32[16,256,1408]{2,1,0:T(8,128)} %param.5) | data formatting | bytes 46137344 | tf_op args[0]
  56.2 32.6 %all-reduce.3.cloned.1.call-done = (f32[16,1408]{1,0:T(8,128)}, f32[16,1408]{1,0:T(8,128)}, f32[16,1408]{1,0:T(8,128)}) async-done(((f32[16,1408]{1,0:T(8,128)}, f32[16,1408]{1,0:T(8,128)}, f32[16,1408]{1,0:T(8,128)}), (f32[16,1408]{1,0:T(8,128)}, f32[16,1408]{1,0:T(8,128)}, f32[16,1408]{1,0:T(8,128)})) %all-reduce.3.cloned.1.call-update) | async-done | bytes 270352 | tf_op jit(solution)/shard_map/psum | solution.py:8
  90.0 14.2 %divide_convert_fusion.1 = bf16[16,256,1408]{1,0,2:T(8,128)(2,1)} fusion(f32[16,256,1408]{1,0,2:T(8,128)} %copy.24, f32[16,1408]{0,1:T(8,128)S(1)} %copy.23), kind=kLoop, calls=%fused_computation.5 | loop fusion | flops 11534336 | bytes 34693120 | tf_op jit(solution)/shard_map/convert_element_type | solution.py:20
  104.2 5.2 all-to-all-start
  109.4 23.7 %copy.28 = f32[16,256,1408]{1,0,2:T(8,128)} copy(f32[16,256,1408]{2,1,0:T(8,128)} %param.6) | data formatting | bytes 46137344 | tf_op args[1]
  133.4 14.2 %divide_convert_fusion = bf16[16,256,1408]{1,0,2:T(8,128)(2,1)} fusion(f32[16,256,1408]{1,0,2:T(8,128)} %copy.28, f32[16,1408]{0,1:T(8,128)S(1)} %copy.27), kind=kLoop, calls=%fused_computation.3 | loop fusion | flops 11534336 | bytes 34693120 | tf_op jit(solution)/shard_map/convert_element_type | solution.py:21
  147.7 89.5 %all-to-all-done = bf16[16,256,1408]{1,0,2:T(8,128)(2,1)} async-done(((bf16[16,256,1408]{1,0,2:T(8,128)(2,1)}), bf16[16,256,1408]{1,0,2:T(8,128)(2,1)}, u32[]{:S(2)}, u32[]{:S(2)}) %all-to-all-start) | async-done | bytes 11534368 | tf_op jit(solution)/shard_map/all_to_all | solution.py:25
  237.2 5.3 all-to-all-start.1
  242.8 32.6 %fusion = bf16[16,1408,256]{2,0,1:T(8,128)(2,1)} fusion(f32[16,1408,256]{2,1,0:T(8,128)} %param.7, f32[16,1408]{0,1:T(8,128)S(1)} %copy.31), kind=kLoop, calls=%fused_computation.1 | loop fusion | flops 11534336 | bytes 34693120 | tf_op jit(solution)/shard_map/convert_element_type | solution.py:22
  275.4 94.8 %all-to-all-done.1 = bf16[16,256,1408]{1,0,2:T(8,128)(2,1)} async-done(((bf16[16,256,1408]{1,0,2:T(8,128)(2,1)}), bf16[16,256,1408]{1,0,2:T(8,128)(2,1)}, u32[]{:S(2)}, u32[]{:S(2)}) %all-to-all-start.1) | async-done | bytes 11534368 | tf_op jit(solution)/shard_map/all_to_all | solution.py:26
  370.2 5.3 all-to-all-start.2
  375.9 126.8 %collective-permute-done = bf16[256,16]{0,1:T(8,128)(2,1)S(1)} collective-permute-done((bf16[256,16]{0,1:T(8,128)(2,1)S(1)}, bf16[256,16]{0,1:T(8,128)(2,1)S(1)}, u32[]{:S(2)}, u32[]{:S(2)}) %collective-permute-start) | collective-permute-done | bytes 8224 | tf_op jit(solution)/shard_map/ppermute | solution.py:41
  502.7 4.0 collective-permute-done.1
  506.7 4.0 collective-permute-done.2
  526.7 14.6 %all_gather.3 = bf16[2048,64]{0,1:T(8,128)(2,1)S(1)} all-gather(bf16[2048,16]{0,1:T(8,128)(2,1)S(1)} %constant_dynamic-slice_fusion), channel_id=1, replica_groups=mesh['ep'=4,'fsdp'=8] {'ep'}, dimensions={1}, use_global_device_ids=true | all-gather | bytes 327680 | tf_op jit(solution)/shard_map/all_gather | solution.py:45
  543.3 11.3 %copy.26 = bf16[16,8,256,176]{2,1,3,0:T(8,128)(2,1)} copy(bf16[16,8,256,176]{2,0,3,1:T(8,128)(2,1)} %bitcast.2) | data formatting | bytes 23068672 | tf_op jit(solution)/shard_map/all_to_all | solution.py:25
  554.7 18.0 %all_to_all.42 = bf16[16,2048,176]{1,2,0:T(8,128)(2,1)} reshape(bf16[16,8,256,176]{2,1,3,0:T(8,128)(2,1)} %copy.26) | data formatting | bytes 23068672 | tf_op jit(solution)/shard_map/all_to_all | solution.py:25
  572.6 11.3 %copy.30 = bf16[16,8,256,176]{2,1,3,0:T(8,128)(2,1)} copy(bf16[16,8,256,176]{2,0,3,1:T(8,128)(2,1)} %bitcast.5) | data formatting | bytes 23068672 | tf_op jit(solution)/shard_map/all_to_all | solution.py:26
  584.0 18.0 %all_to_all.46 = bf16[16,2048,176]{1,2,0:T(8,128)(2,1)} reshape(bf16[16,8,256,176]{2,1,3,0:T(8,128)(2,1)} %copy.30) | data formatting | bytes 23068672 | tf_op jit(solution)/shard_map/all_to_all | solution.py:26
  601.9 11.4 %copy.33 = bf16[16,176,8,256]{3,2,1,0:T(8,128)(2,1)} copy(bf16[16,176,8,256]{3,0,1,2:T(8,128)(2,1)} %bitcast.7) | data formatting | bytes 23068672 | tf_op jit(solution)/shard_map/all_to_all | solution.py:28
  613.3 18.0 %all_to_all.50 = bf16[16,176,2048]{2,1,0:T(8,128)(2,1)} reshape(bf16[16,176,8,256]{3,2,1,0:T(8,128)(2,1)} %copy.33) | data formatting | bytes 23068672 | tf_op jit(solution)/shard_map/all_to_all | solution.py:28
  (51 shorter events, 21.0 us)
Async XLA Ops:
  7.2 81.6 %all-reduce.3.cloned.1.call-start = ((), (), s32[]{:S(2)}) async-start(), calls=%async_computation.3 | async-start | bytes 540672 | tf_op jit(solution)/shard_map/psum | solution.py:8
  7.2 14.2 %copy-start = (f32[16,256,1408]{2,1,0:T(8,128)S(1)}, f32[16,256,1408]{2,1,0:T(8,128)}, u32[]{:S(2)}) copy-start(f32[16,256,1408]{2,1,0:T(8,128)} %param.5) | copy-start | bytes 69206016
  104.2 133.0 %all-to-all-start = ((bf16[16,256,1408]{1,0,2:T(8,128)(2,1)}), bf16[16,256,1408]{1,0,2:T(8,128)(2,1)}, u32[]{:S(2)}, u32[]{:S(2)}) async-start(bf16[16,256,1408]{1,0,2:T(8,128)(2,1)} %divide_convert_fusion.1), calls=%async_computation | async-start | bytes 23068672 | tf_op jit(solution)/shard_map/all_to_all | solution.py:25
  109.4 23.7 %copy-start.3 = (f32[16,1408]{1,0:T(8,128)S(1)}, f32[16,1408]{1,0:T(8,128)}, u32[]{:S(2)}) copy-start(f32[16,1408]{1,0:T(8,128)} %get-tuple-element.8) | copy-start | bytes 270340
  133.4 109.0 %copy-start.2 = (f32[16,1408]{1,0:T(8,128)S(1)}, f32[16,1408]{1,0:T(8,128)}, u32[]{:S(2)}) copy-start(f32[16,1408]{1,0:T(8,128)} %get-tuple-element.9) | copy-start | bytes 270340
  237.2 133.0 %all-to-all-start.1 = ((bf16[16,256,1408]{1,0,2:T(8,128)(2,1)}), bf16[16,256,1408]{1,0,2:T(8,128)(2,1)}, u32[]{:S(2)}, u32[]{:S(2)}) async-start(bf16[16,256,1408]{1,0,2:T(8,128)(2,1)} %divide_convert_fusion), calls=%async_computation.1 | async-start | bytes 23068672 | tf_op jit(solution)/shard_map/all_to_all | solution.py:26
  242.7 132.7 %copy-start.1 = (f32[256,16]{0,1:T(8,128)S(1)}, f32[256,16]{0,1:T(8,128)}, u32[]{:S(2)}) copy-start(f32[256,16]{0,1:T(8,128)} %param.8) | copy-start | bytes 49156
  242.7 132.7 %copy-start.4 = (f32[256]{0:T(256)S(1)}, f32[256]{0:T(256)}, u32[]{:S(2)}) copy-start(f32[256]{0:T(256)} %param.9) | copy-start | bytes 3076
  370.2 231.8 %all-to-all-start.2 = ((bf16[16,1408,256]{2,0,1:T(8,128)(2,1)}), bf16[16,1408,256]{2,0,1:T(8,128)(2,1)}, u32[]{:S(2)}, u32[]{:S(2)}) async-start(bf16[16,1408,256]{2,0,1:T(8,128)(2,1)} %fusion), calls=%async_computation.2 | async-start | bytes 23068672 | tf_op jit(solution)/shard_map/all_to_all | solution.py:28
  375.5 127.2 %collective-permute-start = (bf16[256,16]{0,1:T(8,128)(2,1)S(1)}, bf16[256,16]{0,1:T(8,128)(2,1)S(1)}, u32[]{:S(2)}, u32[]{:S(2)}) collective-permute-start(bf16[256,16]{0,1:T(8,128)(2,1)S(1)} %multiply_convert_fusion), channel_id=1, source_target_pairs={{0,1},{1,2},{2,3},{3,4},{4,5},{5,6},{6,7},{7,0},{8,9},{9,10},{10,1... | collective-permute-start | bytes 24584 | tf_op jit(solution)/shard_map/ppermute | solution.py:41
  502.7 4.0 collective-permute-start.1
  506.7 4.0 collective-permute-start.2
  510.7 4.0 collective-permute-start.3
  514.6 4.0 collective-permute-start.4
  518.6 4.0 collective-permute-start.5
  522.6 4.0 collective-permute-start.6
Sparse Core Ops, SparseCore 0:
  32.6 56.1 all-reduce.2
